TPU v7x, 32 devices: a 4x4x1 block of a 4x4x8 slice. The times are simulated.
32 devices in a mesh: data: 1 (over z), expert: 32 (over y, x, core).
Axes of the slice: x: 4, y: 4, z: 1, core: 2. Of those that a mesh axis runs over, the one named last changes fastest.
The devices are a block of a 4x4x8 slice.
Arguments:
- x: bfloat16 [8192, 2048], P(('data', 'expert'))
- idx: int32 [8192, 8], P(('data', 'expert'))
- g: float32 [8192, 8], P(('data', 'expert'))
- hot_tok: int32 [1024], P(('data', 'expert'))
- W1: bfloat16 [128, 2048, 768], P('expert')
- W3: bfloat16 [128, 2048, 768], P('expert')
- W2: bfloat16 [128, 768, 2048], P('expert')
Outputs:
- output: bfloat16 [8192, 2048], P(('data', 'expert'))
All inputs are finite; a program needn't handle non-finite values.
Results may differ from a plain program's by a relative error of at most 0.001.
Values are sent between devices in bfloat16 or wider.
A program may use at most 768 MiB of HBM per device.

v0:
```python
import jax
import jax.numpy as jnp
from jax import lax
from jax.sharding import PartitionSpec as P


def _dest(idx, hot_tok, n, el, ch, cap):
    t, k = idx.shape
    s = ch + (el - 1) * cap
    flat = idx.reshape(-1)
    onehot = (flat[:, None] == jnp.arange(n * el, dtype=jnp.int32)[None, :]).astype(jnp.int32)
    rank = jnp.take_along_axis(jnp.cumsum(onehot, axis=0) - onehot, flat[:, None], axis=1).reshape(t, k)
    hot_rank = jnp.zeros((t,), jnp.int32).at[hot_tok].set(jnp.arange(ch, dtype=jnp.int32))
    loc = idx % el
    pos = (idx // el) * s + jnp.where(loc == 0, rank, ch + (loc - 1) * cap + rank)
    return jnp.where(idx == 0, hot_rank[:, None], pos)


def _send(x, dest, rows):
    t, d = x.shape
    k = dest.shape[1]
    src = jnp.full((rows,), t, jnp.int32).at[dest.reshape(-1)].set(jnp.repeat(jnp.arange(t, dtype=jnp.int32), k))
    return jnp.concatenate([x, jnp.zeros((1, d), x.dtype)])[src]


def _combine(back, dest, g):
    y = jnp.zeros((dest.shape[0], back.shape[1]), jnp.float32)
    for j in range(dest.shape[1]):
        y = y + g[:, j:j + 1] * back[dest[:, j]].astype(jnp.float32)
    return y.astype(jnp.bfloat16)


def _experts(xs, w1, w3, w2, form_in, form_out):
    a = jnp.einsum(form_in, xs, w1, preferred_element_type=jnp.float32)
    b = jnp.einsum(form_in, xs, w3, preferred_element_type=jnp.float32)
    u = (jax.nn.silu(a) * b).astype(jnp.bfloat16)
    return jnp.einsum(form_out, u, w2, preferred_element_type=jnp.float32).astype(jnp.bfloat16)


def solution(mesh):
    n = mesh.shape['expert']

    def local(x, idx, g, hot_tok, w1, w3, w2):
        t, d = x.shape
        k = idx.shape[1]
        el = w1.shape[0]
        e = el * n
        ch = hot_tok.shape[0]
        cap = 2 * ((t * k - ch + e - 2) // (e - 1))
        s = ch + (el - 1) * cap
        dest = _dest(idx, hot_tok, n, el, ch, cap)
        send = _send(x, dest, n * s).reshape(n, s, d)
        recv = lax.all_to_all(send, 'expert', 0, 0, tiled=True)
        out = _experts(recv[:, :ch], w1[0], w3[0], w2[0], 'rcd,df->rcf', 'rcf,fd->rcd')
        if el > 1:
            xc = recv[:, ch:].reshape(n, el - 1, cap, d)
            oc = _experts(xc, w1[1:], w3[1:], w2[1:], 'recd,edf->recf', 'recf,efd->recd')
            out = jnp.concatenate([out, oc.reshape(n, (el - 1) * cap, d)], axis=1)
        back = lax.all_to_all(out, 'expert', 0, 0, tiled=True)
        return _combine(back.reshape(n * s, d), dest, g)

    rows = P(('data', 'expert'))
    wspec = P('expert')
    return jax.shard_map(local, mesh=mesh, in_specs=(rows, rows, rows, rows, wspec, wspec, wspec), out_specs=rows, check_vma=False)
```

profile of v0, /device:TPU:107, one launch (start us, length us, event | category | flops | bytes accessed | tf_op | source)
XLA Modules:
  0.0 689.8 jit_solution(4216539018258261522)
XLA Ops:
  1.4 0.8 copy.27
  5.2 16.8 %gather_fusion.9 = s32[2048]{0:T(1024)S(1)} fusion(s32[2048,128]{0,1:T(8,128)S(1)} %bitcast_subtract_fusion, s32[2048]{0:T(1024)S(1)} %bitcast.81), kind=kCustom, calls=%fused_computation.9 | custom fusion | bytes 32768 | tf_op jit(solution)/shard_map/jit(take_along_axis)/gather | solution.py:12
  23.1 8.1 %scatter_custom_fusion.1 = s32[4096]{0:T(1024)S(1)} fusion(s32[2048]{0:T(1024)S(1)} %bitcast.87, s32[2048]{0:T(1024)S(1)} %reshape.239, s32[]{:T(128)} %constant.41.clone.1), kind=kCustom, calls=%fused_computation.92 | custom fusion | bytes 16388 | tf_op jit(solution)/shard_map/scatter | solution.py:22
  31.3 21.0 %gather_fusion = bf16[4096,2048]{1,0:T(8,128)(2,1)} fusion(bf16[257,2048]{1,0:T(8,128)(2,1)S(1)} %concatenate.6, s32[4096]{0:T(1024)S(1)} %fusion.61), kind=kCustom, calls=%fused_computation | custom fusion | bytes 33570816 | tf_op jit(solution)/shard_map/gather | solution.py:23
  52.2 206.9 %all_to_all.10 = bf16[32,128,2048]{2,1,0:T(8,128)(2,1)S(1)} all-to-all(bf16[32,128,2048]{2,1,0:T(8,128)(2,1)} %bitcast.82), channel_id=1, replica_groups=mesh['data'=1,'expert'=32] {'expert'}, dimensions={0} | all-to-all | bytes 33554432 | tf_op jit(solution)/shard_map/all_to_all | solution.py:53
  259.1 6.4 slice.129
  265.5 3.1 copy-done
  268.6 17.8 %fusion = f32[3,32,32,768]{3,2,1,0:T(8,128)} fusion(bf16[32,3,32,2048]{3,2,1,0:T(8,128)(2,1)} %bitcast.84, bf16[4,2048,768]{2,1,0:T(8,128)(2,1)} %param.12), kind=kOutput, calls=%fused_computation.14 | convolution fusion | flops 9663676416 | bytes 31457280 | tf_op jit(solution)/shard_map/recd,edf->recf/dot_general | solution.py:35
  286.4 29.9 %convert_bitcast_fusion = bf16[32,3,32,2048]{3,2,0,1:T(8,128)(2,1)} fusion(bf16[4,768,2048]{2,1,0:T(8,128)(2,1)} %param.13, f32[3,32,32,768]{3,2,1,0:T(8,128)} %fusion, bf16[32,3,32,2048]{3,2,1,0:T(8,128)(2,1)} %bitcast.85, bf16[4,2048,768]{2,1,0:T(8,128)(2,1)} %param.11), kind=kOutput, calls=%fused_computation.13 | convolution fusion | flops 19347800064 | bytes 53477376 | tf_op jit(solution)/shard_map/recf,efd->recd/dot_general | solution.py:37
  316.2 10.7 %copy.43 = bf16[32,3,32,2048]{3,2,1,0:T(8,128)(2,1)} copy(bf16[32,3,32,2048]{3,2,0,1:T(8,128)(2,1)} %convert_bitcast_fusion) | data formatting | bytes 25165824 | tf_op jit(solution)/shard_map/convert_element_type | solution.py:37
  326.9 6.1 fusion.21
  333.1 12.8 %convolution_convert_fusion = bf16[32,32,2048]{2,1,0:T(8,128)(2,1)} fusion(bf16[4,768,2048]{2,1,0:T(8,128)(2,1)} %param.13, f32[32,32,768]{2,1,0:T(8,128)S(1)} %fusion.21, bf16[4,2048,768]{2,1,0:T(8,128)(2,1)} %param.12, bf16[32,128,2048]{2,1,0:T(8,128)(2,1)} %copy-done), kind=kOutput, calls=%fused_computation.33 | convolution fusion | flops 6449266688 | bytes 17825792 | tf_op jit(solution)/shard_map/rcf,fd->rcd/dot_general | solution.py:37
  345.8 13.8 %pad_maximum_fusion = bf16[32,128,2048]{2,1,0:T(8,128)(2,1)} fusion(bf16[32,96,2048]{2,1,0:T(8,128)(2,1)} %bitcast.83, bf16[32,32,2048]{2,1,0:T(8,128)(2,1)} %convolution_convert_fusion), kind=kLoop, calls=%fused_computation.12 | loop fusion | flops 33554432 | bytes 33554432 | tf_op jit(solution)/shard_map/concatenate | solution.py:58
  359.7 14.5 %all-to-all-start.1 = ((bf16[32,128,2048]{2,1,0:T(8,128)(2,1)}), bf16[32,128,2048]{2,1,0:T(8,128)(2,1)}, u32[]{:S(2)}, u32[]{:S(2)}) async-start(bf16[32,128,2048]{2,1,0:T(8,128)(2,1)} %pad_maximum_fusion), calls=%async_computation.1 | async-start | bytes 33554432 | tf_op jit(solution)/shard_map/all_to_all | solution.py:59
  374.9 222.6 %all-to-all-done.1 = bf16[32,128,2048]{2,1,0:T(8,128)(2,1)} async-done(((bf16[32,128,2048]{2,1,0:T(8,128)(2,1)}), bf16[32,128,2048]{2,1,0:T(8,128)(2,1)}, u32[]{:S(2)}, u32[]{:S(2)}) %all-to-all-start.1) | async-done | bytes 16777248 | tf_op jit(solution)/shard_map/all_to_all | solution.py:59
  597.6 10.3 %gather_fusion.8 = bf16[256,2048]{1,0:T(8,128)(2,1)S(1)} fusion(bf16[4096,2048]{1,0:T(8,128)(2,1)} %bitcast.25, s32[1024]{0:T(1024)S(1)} %get-tuple-element.21), kind=kCustom, calls=%fused_computation.8 | custom fusion | bytes 2098176 | tf_op jit(solution)/shard_map/gather | solution.py:29
  607.9 10.3 %gather_fusion.7 = bf16[256,2048]{1,0:T(8,128)(2,1)S(1)} fusion(bf16[4096,2048]{1,0:T(8,128)(2,1)} %bitcast.25, s32[1024]{0:T(1024)S(1)} %get-tuple-element.22), kind=kCustom, calls=%fused_computation.7 | custom fusion | bytes 2098176 | tf_op jit(solution)/shard_map/gather | solution.py:29
  618.1 10.5 %gather_fusion.6 = bf16[256,2048]{1,0:T(8,128)(2,1)S(1)} fusion(bf16[4096,2048]{1,0:T(8,128)(2,1)} %bitcast.25, s32[1024]{0:T(1024)S(1)} %get-tuple-element.23), kind=kCustom, calls=%fused_computation.6 | custom fusion | bytes 2098176 | tf_op jit(solution)/shard_map/gather | solution.py:29
  628.6 11.3 %gather_fusion.5 = bf16[256,2048]{1,0:T(8,128)(2,1)} fusion(bf16[4096,2048]{1,0:T(8,128)(2,1)} %bitcast.25, s32[1024]{0:T(1024)S(1)} %get-tuple-element.24), kind=kCustom, calls=%fused_computation.5 | custom fusion | bytes 2098176 | tf_op jit(solution)/shard_map/gather | solution.py:29
  639.9 11.3 %gather_fusion.4 = bf16[256,2048]{1,0:T(8,128)(2,1)} fusion(bf16[4096,2048]{1,0:T(8,128)(2,1)} %bitcast.25, s32[1024]{0:T(1024)S(1)} %get-tuple-element.25), kind=kCustom, calls=%fused_computation.4 | custom fusion | bytes 2098176 | tf_op jit(solution)/shard_map/gather | solution.py:29
  651.2 11.5 %gather_fusion.3 = bf16[256,2048]{1,0:T(8,128)(2,1)} fusion(bf16[4096,2048]{1,0:T(8,128)(2,1)} %bitcast.25, s32[1024]{0:T(1024)S(1)} %get-tuple-element.26), kind=kCustom, calls=%fused_computation.3 | custom fusion | bytes 2098176 | tf_op jit(solution)/shard_map/gather | solution.py:29
  662.7 11.3 %gather_fusion.2 = bf16[256,2048]{1,0:T(8,128)(2,1)} fusion(bf16[4096,2048]{1,0:T(8,128)(2,1)} %bitcast.25, s32[1024]{0:T(1024)S(1)} %get-tuple-element.27), kind=kCustom, calls=%fused_computation.2 | custom fusion | bytes 2098176 | tf_op jit(solution)/shard_map/gather | solution.py:29
  674.0 11.3 %gather_fusion.1 = bf16[256,2048]{1,0:T(8,128)(2,1)} fusion(bf16[4096,2048]{1,0:T(8,128)(2,1)} %bitcast.25, s32[1024]{0:T(1024)S(1)} %get-tuple-element.28), kind=kCustom, calls=%fused_computation.1 | custom fusion | bytes 2098176 | tf_op jit(solution)/shard_map/gather | solution.py:29
  685.2 4.3 add_convert_fusion
  (46 shorter events, 6.1 us)
Async XLA Ops:
  4.2 27.0 %copy-start.3 = (bf16[256,2048]{1,0:T(8,128)(2,1)S(1)}, bf16[256,2048]{1,0:T(8,128)(2,1)}, u32[]{:S(2)}) copy-start(bf16[256,2048]{1,0:T(8,128)(2,1)} %param.7) | copy-start | bytes 3145732
  22.9 8.2 %copy-start.1 = (s32[256,8]{1,0:T(8,128)}, s32[256,8]{1,0:T(8,128)S(1)}, u32[]{:S(2)}) copy-start(s32[256,8]{1,0:T(8,128)S(1)} %fusion.50) | copy-start | bytes 24580
  259.1 9.5 %copy-start = (bf16[32,128,2048]{2,1,0:T(8,128)(2,1)}, bf16[32,128,2048]{2,1,0:T(8,128)(2,1)S(1)}, u32[]{:S(2)}) copy-start(bf16[32,128,2048]{2,1,0:T(8,128)(2,1)S(1)} %all_to_all.10) | copy-start | bytes 50331652
  359.7 14.6 %copy-start.2 = (s32[256,8]{1,0:T(8,128)S(1)}, s32[256,8]{1,0:T(8,128)}, u32[]{:S(2)}) copy-start(s32[256,8]{1,0:T(8,128)} %copy-done.1) | copy-start | bytes 24580
  359.7 15.2 %copy-start.4 = (f32[256,8]{0,1:T(8,128)S(1)}, f32[256,8]{0,1:T(8,128)}, u32[]{:S(2)}) copy-start(f32[256,8]{0,1:T(8,128)} %param.9) | copy-start | bytes 24580
  359.7 237.9 %all-to-all-start.1 = ((bf16[32,128,2048]{2,1,0:T(8,128)(2,1)}), bf16[32,128,2048]{2,1,0:T(8,128)(2,1)}, u32[]{:S(2)}, u32[]{:S(2)}) async-start(bf16[32,128,2048]{2,1,0:T(8,128)(2,1)} %pad_maximum_fusion), calls=%async_computation.1 | async-start | bytes 33554432 | tf_op jit(solution)/shard_map/all_to_all | solution.py:59
where the time goes:
time: 695 us; the launch traced here: 690 us
  waiting for transfers between devices  223 us (32%)
  blocking collectives  207 us (30%)
  local copies, waits for them, and re-layouts  157 us (23%)
  matrix products  66.6 us (10%)
  other arithmetic  21.7 us (3%)
  starting transfers between devices  14.5 us (2%)
    all_to_all x1, waiting for transfers between devices, local(): back = lax.all_to_all(out, 'expert', 0, 0, tiled=True)  223 us
    all_to_all x1, blocking collectives, local(): recv = lax.all_to_all(send, 'expert', 0, 0, tiled=True)  207 us
    gather x8, local copies, waits for them, and re-layouts, _combine(): y = y + g[:, j:j + 1] * back[dest[:, j]].astype(jnp.float32)  87.6 us
    dot_general x2, matrix products, _experts(): jnp.einsum(form_out, u, w2, preferred_element_type=jnp.float32)  42.6 us
    gather x1, local copies, waits for them, and re-layouts, _send(): return jnp.concatenate([x, jnp.zeros((1, d), x.dtype)])[src]  21 us
    dot_general x1, matrix products, _experts(): b = jnp.einsum(form_in, xs, w3, preferred_element_type=jnp.float32)  17.8 us
    gather x2, local copies, waits for them, and re-layouts, _dest(): jnp.take_along_axis(jnp.cumsum(onehot, axis=0) - onehot, flat[:, None], a...  16.9 us
    all_to_all x1, starting transfers between devices, local(): back = lax.all_to_all(out, 'expert', 0, 0, tiled=True)  14.5 us
  transfers between devices with their start and end apart: 1, of which 1 were waited for; matrix products, arithmetic and copies ran while one was open for 0% of the time, Pallas kernels for 0%

commit v1 on v0

v1 whole, which is shorter than its diff:
```python
import functools
import math

import jax
import jax.numpy as jnp
from jax import lax
from jax.experimental import pallas as pl
from jax.experimental.pallas import tpu as pltpu
from jax.sharding import PartitionSpec as P

MESH = pl.DeviceIdType.MESH
F32 = jnp.float32
BF16 = jnp.bfloat16
ND = 4


def _where(n):
    me = lax.axis_index('expert')
    c = me % 2
    chip = me // 2
    return me, c, chip % ND, chip // ND


def _chip(k, p, q):
    p = p % ND
    q = q % ND
    return (1 - k) * (q * ND + p) + k * (p * ND + q)


def _near(j):
    return j + j // 2 - 2 * (j // 3)


def _greet(devs):
    bar = pltpu.get_barrier_semaphore()
    for dev in devs:
        pl.semaphore_signal(bar, inc=1, device_id={'expert': dev}, device_id_type=MESH)
    pl.semaphore_wait(bar, len(devs))


def _dispatch_kernel(n, el, cap, x_ref, meta_ref, w1_ref, w3_ref, w2_ref, h_ref, xall,
                     w1v, w3v, w2v, xb, xg, uv, hb, wsem, bsem, osem, ssem, rsem):
    t, d = x_ref.shape
    f = w1v.shape[2]
    r = el * cap
    me, c, cx, cy = _where(n)
    o = 1 - c
    p = o * cx + c * cy
    q = o * cy + c * cx
    partner = me + 1 - 2 * c

    def dev(pp, qq):
        return _chip(c, pp, qq) * 2 + c

    _greet([dev(p + 1, q), dev(p - 1, q), dev(p, q + 1), dev(p, q - 1), partner])

    loads = []
    for i, (a, b) in enumerate(((w1_ref, w1v), (w3_ref, w3v), (w2_ref, w2v))):
        loads.append(pltpu.make_async_copy(a, b, wsem.at[i]))
    sends = []

    def part(ref, half):
        return ref if half is None else ref.at[pl.ds(half * (t // 2), t // 2)]

    def send(b, ref, half, to):
        cp = pltpu.make_async_remote_copy(
            src_ref=part(ref, half), dst_ref=part(xall.at[b], half), send_sem=ssem.at[len(sends)],
            recv_sem=rsem.at[b, half or 0], device_id={'expert': to}, device_id_type=MESH)
        cp.start()
        sends.append(cp)

    def arrived(b, half):
        pltpu.make_async_remote_copy(
            src_ref=part(xall.at[b], half), dst_ref=part(xall.at[b], half), send_sem=ssem.at[0],
            recv_sem=rsem.at[b, half or 0], device_id={'expert': partner}, device_id_type=MESH).wait_recv()

    for to in (dev(p + 1, q), dev(p - 1, q), dev(p, q + 1), dev(p, q - 1), partner):
        send(me, x_ref, None, to)
    for cp in loads:
        cp.start()

    def spread(b):
        for to in (dev(p, q + 1), dev(p, q - 1), partner):
            send(b, xall.at[b], None, to)

    b = dev(p + 1, q)
    arrived(b, None)
    send(b, xall.at[b], 1, dev(p - 1, q))
    spread(b)
    b = dev(p - 1, q)
    arrived(b, None)
    send(b, xall.at[b], 0, dev(p + 1, q))
    spread(b)
    b = dev(p + 2, q)
    arrived(b, 0)
    arrived(b, 1)
    spread(b)

    def member(g, i):
        if g == 0:
            return _near(i), 0
        if g == 3:
            return _near(i), 2
        return _near(2 * (g - 1) + i // 2), 1 + 2 * (i % 2)

    def source(g, i, own):
        dp, dq = member(g, i)
        if own:
            return dev(p + dp, q + dq)
        return _chip(o, q + dp, p + dq) * 2 + o

    rows = lax.broadcasted_iota(jnp.int32, (r, t), 0)
    nf = f // 3
    dt = d // 4

    def compute(g):
        for i in range(4):
            src = source(g, i, True)
            ref = x_ref if (g == 0 and i == 0) else xall.at[src]
            pltpu.make_async_copy(ref, xb.at[i], bsem.at[i]).start()
        for i in range(4):
            src = source(g, i, False)
            arrived(src, None)
            pltpu.make_async_copy(xall.at[src], xb.at[4 + i], bsem.at[4 + i]).start()

        def select(own):
            def body(i, carry):
                slot = i if own else 4 + i
                pltpu.make_async_copy(x_ref, xb.at[slot], bsem.at[slot]).wait()
                src = source(g, i, own)
                code = meta_ref[src].astype(jnp.int32) - me * r
                sel = jnp.zeros((r, t), F32)
                for j in range(8):
                    sel = sel + jnp.where(rows == code[j:j + 1, :], 1.0, 0.0)
                xs = jnp.dot(sel.astype(BF16), xb[slot], preferred_element_type=F32).astype(BF16)
                xg[:, pl.ds(slot * cap, cap), :] = xs.reshape(el, cap, d)
                return carry
            lax.fori_loop(0, 4, body, 0)
        select(True)
        select(False)
        if g == 0:
            for cp in loads:
                cp.wait()

        def expert(e, carry):
            def up(m, carry):
                cols = pl.ds(pl.multiple_of(m * nf, nf), nf)
                a = jnp.dot(xg[e], w1v[e, :, cols], preferred_element_type=F32)
                b = jnp.dot(xg[e], w3v[e, :, cols], preferred_element_type=F32)
                uv[:, cols] = (a * jax.nn.sigmoid(a) * b).astype(BF16)
                return carry
            lax.fori_loop(0, 3, up, 0)
            slot = e % 2

            def flush():
                for i in range(8):
                    pltpu.make_async_copy(hb.at[slot, pl.ds(i * cap, cap)], h_ref.at[0, pl.ds(0, cap)],
                                          osem.at[slot, i]).wait()
            if g > 0:
                flush()
            else:
                pl.when(e >= 2)(flush)

            def down(m, carry):
                cols = pl.ds(pl.multiple_of(m * dt, dt), dt)
                hb[slot, :, cols] = jnp.dot(uv[...], w2v[e, :, cols], preferred_element_type=F32).astype(BF16)
                return carry
            lax.fori_loop(0, 4, down, 0)
            for i in range(8):
                src = source(g, i % 4, i < 4)
                pltpu.make_async_copy(hb.at[slot, pl.ds(i * cap, cap)], h_ref.at[src, pl.ds(e * cap, cap)],
                                      osem.at[slot, i]).start()
            return carry
        lax.fori_loop(0, el, expert, 0)

    compute(0)
    for g in (1, 2):
        for i in range(4):
            b = source(g, i, True)
            arrived(b, None)
            if i % 2 == 0:
                send(b, xall.at[b], 1, dev(p, q - 1))
            else:
                send(b, xall.at[b], 0, dev(p, q + 1))
            send(b, xall.at[b], None, partner)
        compute(g)
    for i in range(4):
        b = source(3, i, True)
        arrived(b, 0)
        arrived(b, 1)
        send(b, xall.at[b], None, partner)
    compute(3)
    for slot in range(2):
        for i in range(8):
            pltpu.make_async_copy(hb.at[slot, pl.ds(i * cap, cap)], h_ref.at[0, pl.ds(0, cap)],
                                  osem.at[slot, i]).wait()
    for cp in sends:
        cp.wait_send()


def _return_kernel(n, r, h_ref, meta_ref, y_ref, rx, fwd, acc, r2, r1, gs, ssem, xsem, fsem, sem2, sem1):
    t, d = y_ref.shape
    me, c, cx, cy = _where(n)
    partner = me + 1 - 2 * c
    hr = r // 2
    ht = t // 2
    offs = (2, 1, 3, 0)
    greet = [partner]
    for k in (0, 1):
        pk, qk = (cx, cy) if k == 0 else (cy, cx)
        for s in (1, -1):
            for core in (0, 1):
                greet.append(_chip(k, pk, qk + s) * 2 + core)
    _greet(greet)
    sends = []

    def rcopy(src, dst, sem, to):
        cp = pltpu.make_async_remote_copy(src_ref=src, dst_ref=dst, send_sem=ssem.at[len(sends)], recv_sem=sem,
                                          device_id={'expert': to}, device_id_type=MESH)
        cp.start()
        sends.append(cp)

    def frame(k):
        return (cx, cy) if k == 0 else (cy, cx)

    def give(j):
        for k in (0, 1):
            pk, qk = frame(k)

            def rows(dq):
                return h_ref.at[_chip(k, pk + offs[j], qk + dq) * 2 + k]
            for s, dirn in ((1, 0), (-1, 1)):
                rcopy(rows(2).at[pl.ds(dirn * hr, hr)], fwd.at[k, dirn, j], fsem.at[k, dirn, j],
                      _chip(k, pk, qk + s) * 2 + c)
            for s, slot in ((1, 3), (-1, 1)):
                rcopy(rows(s), rx.at[j, slot, c], xsem.at[j, slot, c, 0], _chip(k, pk, qk + s) * 2 + k)
            far = pltpu.make_async_remote_copy(
                src_ref=rows(0), dst_ref=rx.at[j, 0, c], send_sem=ssem.at[len(sends)], recv_sem=xsem.at[j, 0, c, 0],
                device_id={'expert': partner}, device_id_type=MESH)
            here = pltpu.make_async_copy(rows(0), rx.at[j, 0, c], xsem.at[j, 0, c, 0])
            pl.when(c == k)(lambda: here.start())
            pl.when(c != k)(lambda: far.start())
            sends.append((k, far))

    def relay(j):
        for k in (0, 1):
            pk, qk = frame(k)
            for dirn, s in ((0, 1), (1, -1)):
                buf = fwd.at[k, dirn, j]
                pltpu.make_async_remote_copy(src_ref=buf, dst_ref=buf, send_sem=ssem.at[0],
                                             recv_sem=fsem.at[k, dirn, j], device_id={'expert': partner},
                                             device_id_type=MESH).wait_recv()
                rcopy(buf, rx.at[j, 2, c, pl.ds(dirn * hr, hr)], xsem.at[j, 2, c, dirn],
                      _chip(k, pk, qk + s) * 2 + k)

    o = 1 - c
    p = o * cx + c * cy
    q = o * cy + c * cx

    def collect(j):
        for slot in range(4):
            for core in (0, 1):
                if slot == 2:
                    for half in (0, 1):
                        pltpu.make_async_copy(h_ref.at[0, pl.ds(0, hr)], rx.at[j, slot, core, pl.ds(half * hr, hr)],
                                              xsem.at[j, slot, core, half]).wait()
                else:
                    pltpu.make_async_copy(h_ref.at[0], rx.at[j, slot, core], xsem.at[j, slot, core, 0]).wait()
        src = _chip(c, p + offs[j], q) * 2 + c
        meta = meta_ref[src].T
        lanes = lax.broadcasted_iota(jnp.int32, (t, r), 1)
        code = meta[:, :8].astype(jnp.int32)
        for slot in range(4):
            for core in (0, 1):
                base = (_chip(c, p, q + slot) * 2 + core) * r
                gm = jnp.zeros((t, r), F32)
                for i in range(8):
                    gm = gm + jnp.where(code[:, i:i + 1] - base == lanes, meta[:, 8 + i:9 + i], 0.0)
                hi = gm.astype(BF16)
                rest = gm - hi.astype(F32)
                mid = rest.astype(BF16)
                low = (rest - mid.astype(F32)).astype(BF16)
                cols = pl.ds((slot * 2 + core) * r, r)
                gs[0, :, cols] = hi
                gs[1, :, cols] = mid
                gs[2, :, cols] = low
        dt = d // 4

        def tile(m, carry):
            cols = pl.ds(pl.multiple_of(m * dt, dt), dt)
            rhs = rx[j, :, :, :, cols].reshape(8 * r, dt)
            s = jnp.dot(gs[0], rhs, preferred_element_type=F32)
            s = s + jnp.dot(gs[1], rhs, preferred_element_type=F32)
            s = s + jnp.dot(gs[2], rhs, preferred_element_type=F32)
            acc[j, :, cols] = s
            return carry
        lax.fori_loop(0, 4, tile, 0)

    def wait2(i):
        pltpu.make_async_remote_copy(src_ref=r2.at[i], dst_ref=r2.at[i], send_sem=ssem.at[0], recv_sem=sem2.at[i],
                                     device_id={'expert': partner}, device_id_type=MESH).wait_recv()

    def wait1(i):
        pltpu.make_async_remote_copy(src_ref=r1.at[i], dst_ref=r1.at[i], send_sem=ssem.at[0], recv_sem=sem1.at[i],
                                     device_id={'expert': partner}, device_id_type=MESH).wait_recv()

    up = _chip(c, p + 1, q) * 2 + c
    down = _chip(c, p - 1, q) * 2 + c
    give(0)
    give(1)
    relay(0)
    give(2)
    collect(0)
    rcopy(acc.at[0, pl.ds(0, ht)], r2.at[0], sem2.at[0], up)
    rcopy(acc.at[0, pl.ds(ht, ht)], r2.at[1], sem2.at[1], down)
    relay(1)
    give(3)
    collect(1)
    wait2(0)
    acc[1, 0:ht] = acc[1, 0:ht] + r2[0]
    rcopy(acc.at[1], r1.at[0], sem1.at[0], up)
    relay(2)
    collect(2)
    wait2(1)
    acc[2, ht:t] = acc[2, ht:t] + r2[1]
    rcopy(acc.at[2], r1.at[1], sem1.at[1], down)
    relay(3)
    collect(3)
    wait1(0)
    wait1(1)
    y_ref[...] = (acc[3] + r1[0] + r1[1]).astype(BF16)
    for cp in sends:
        if isinstance(cp, tuple):
            k, far = cp
            pl.when(c != k)(lambda: far.wait_send())
        else:
            cp.wait_send()


def solution(mesh):
    n = mesh.shape['expert']
    assert n == 2 * ND * ND

    def local(x, idx, g, hot_tok, w1, w3, w2):
        t, d = x.shape
        k = idx.shape[1]
        el, _, f = w1.shape
        e = el * n
        ch = hot_tok.shape[0]
        cap = max(ch, 2 * ((t * k - ch + e - 2) // (e - 1)))
        r = el * cap

        hit = idx[:, :, None] == jnp.arange(e, dtype=jnp.int32)
        chosen = hit.any(axis=1).astype(BF16)
        earlier = (jnp.arange(t)[:, None] > jnp.arange(t)[None, :]).astype(BF16)
        before = jnp.dot(earlier, chosen, preferred_element_type=F32)
        rank = jnp.where(hit, before[:, None, :], 0.0).sum(axis=2)
        code = (idx * cap).astype(F32) + rank
        meta = jnp.concatenate([code.T, g.T], axis=0)
        meta = lax.all_gather(meta, 'expert')

        anyspec = pl.BlockSpec(memory_space=pl.ANY)
        vspec = pl.BlockSpec(memory_space=pltpu.VMEM)
        h, _ = pl.pallas_call(
            functools.partial(_dispatch_kernel, n, el, cap),
            out_shape=[jax.ShapeDtypeStruct((n, r, d), BF16), jax.ShapeDtypeStruct((n, t, d), BF16)],
            in_specs=[anyspec, vspec, anyspec, anyspec, anyspec],
            out_specs=[anyspec, anyspec],
            scratch_shapes=[
                pltpu.VMEM(w1.shape, BF16), pltpu.VMEM(w3.shape, BF16), pltpu.VMEM(w2.shape, BF16),
                pltpu.VMEM((8, t, d), BF16), pltpu.VMEM((el, 8 * cap, d), BF16),
                pltpu.VMEM((8 * cap, f), BF16), pltpu.VMEM((2, 8 * cap, d), BF16),
                pltpu.SemaphoreType.DMA((3,)), pltpu.SemaphoreType.DMA((8,)), pltpu.SemaphoreType.DMA((2, 8)),
                pltpu.SemaphoreType.DMA((36,)), pltpu.SemaphoreType.DMA((n, 2)),
            ],
            compiler_params=pltpu.CompilerParams(collective_id=0, has_side_effects=True,
                                                 vmem_limit_bytes=66_000_000),
        )(x, meta, w1, w3, w2)
        return pl.pallas_call(
            functools.partial(_return_kernel, n, r),
            out_shape=jax.ShapeDtypeStruct((t, d), BF16),
            in_specs=[anyspec, vspec],
            out_specs=vspec,
            scratch_shapes=[
                pltpu.VMEM((4, 4, 2, r, d), BF16), pltpu.VMEM((2, 2, 4, r // 2, d), BF16),
                pltpu.VMEM((4, t, d), F32), pltpu.VMEM((2, t // 2, d), F32), pltpu.VMEM((2, t, d), F32),
                pltpu.VMEM((3, t, 8 * r), BF16),
                pltpu.SemaphoreType.DMA((60,)), pltpu.SemaphoreType.DMA((4, 4, 2, 2)),
                pltpu.SemaphoreType.DMA((2, 2, 4)), pltpu.SemaphoreType.DMA((2,)), pltpu.SemaphoreType.DMA((2,)),
            ],
            compiler_params=pltpu.CompilerParams(collective_id=1, has_side_effects=True,
                                                 vmem_limit_bytes=60_000_000),
        )(h, meta)

    rows = P(('data', 'expert'))
    wspec = P('expert')
    return jax.shard_map(local, mesh=mesh, in_specs=(rows, rows, rows, rows, wspec, wspec, wspec), out_specs=rows,
                         check_vma=False)
```

time: 695 us -> 355 us (0.51)
  the two profiles are of different devices: /device:TPU:107 before, /device:TPU:97 now
where the time goes in v1:
time: 355 us
  Pallas kernels  316 us (89%)
  blocking collectives  32.6 us (9%)
    pallas_call x1, Pallas kernels, local(): pl.pallas_call(functools.partial(_return_kernel, n, r), out_shape=jax.Sha...  171 us
    pallas_call x1, Pallas kernels, local(): pl.pallas_call(functools.partial(_dispatch_kernel, n, el, cap), out_shape...  145 us
    all_gather x1, blocking collectives, local(): meta = lax.all_gather(meta, 'expert')  32.6 us

profile of v1, /device:TPU:97, one launch (start us, length us, event | category | flops | bytes accessed | tf_op | source)
XLA Modules:
  0.0 355.0 jit_solution(865756877391932153)
XLA Ops:
  0.0 0.8 copy.17
  0.8 0.4 fusion
  1.3 0.2 fusion.1
  1.5 0.9 select_reduce_fusion
  2.3 0.1 copy.18
  2.4 0.7 add_bitcast_fusion
  3.1 0.7 pad_maximum_fusion
  3.8 32.6 %all-gather = f32[512,256]{1,0:T(8,128)} all-gather(f32[16,256]{1,0:T(8,128)S(1)} %pad_maximum_fusion), channel_id=2, replica_groups=mesh['data'=1,'expert'=32] {'expert'}, dimensions={0}, use_global_device_ids=true | all-gather | bytes 540672 | tf_op jit(solution)/shard_map/all_gather | solution.py:360
  36.4 145.1 %shard_map.64 = (bf16[32,128,2048]{2,1,0:T(8,128)(2,1)}, bf16[32,256,2048]{2,1,0:T(8,128)(2,1)}) custom-call(bf16[256,2048]{1,0:T(8,128)(2,1)} %x_ref.1, f32[32,16,256]{2,1,0:T(8,128)} %bitcast.5, bf16[4,2048,768]{2,1,0:T(8,128)(2,1)} %w1_ref.1, bf16[4,2048,768]{2,1,0:T(8,128)(2,1)} %w3_ref.1, bf16[4,768,2048]{2,1,0:T(8,128)(2,1)} %w2_ref.1), custom_call_target="tpu_custom_call" | custom-call | tf_op jit(solution)/shard_map/pallas_call | solution.py:364
  181.5 171.2 %shard_map.65 = bf16[256,2048]{1,0:T(8,128)(2,1)} custom-call(bf16[32,128,2048]{2,1,0:T(8,128)(2,1)} %get-tuple-element.6.h_ref, f32[32,16,256]{2,1,0:T(8,128)} %bitcast.6), custom_call_target="tpu_custom_call" | custom-call | tf_op jit(solution)/shard_map/pallas_call | solution.py:379
  352.7 2.3 copy.20

commit v2 on v0

v2 whole, which is shorter than its diff:
```python
import functools
import math

import jax
import jax.numpy as jnp
from jax import lax
from jax.experimental import pallas as pl
from jax.experimental.pallas import tpu as pltpu
from jax.sharding import PartitionSpec as P

MESH = pl.DeviceIdType.MESH
F32 = jnp.float32
BF16 = jnp.bfloat16
ND = 4


def _where(n):
    me = lax.axis_index('expert')
    c = me % 2
    chip = me // 2
    return me, c, chip % ND, chip // ND


def _chip(k, p, q):
    p = p % ND
    q = q % ND
    return (1 - k) * (q * ND + p) + k * (p * ND + q)


def _near(j):
    return j + j // 2 - 2 * (j // 3)


def _greet(devs):
    bar = pltpu.get_barrier_semaphore()
    for dev in devs:
        pl.semaphore_signal(bar, inc=1, device_id={'expert': dev}, device_id_type=MESH)
    pl.semaphore_wait(bar, len(devs))


def _dispatch_kernel(n, el, cap, x_ref, meta_ref, w1_ref, w3_ref, w2_ref, h_ref, xall, metas,
                     w1v, w3v, w2v, xb, xg, uv, hb, wsem, bsem, osem, ssem, rsem, msem, mrsem):
    t, d = x_ref.shape
    f = w1v.shape[2]
    r = el * cap
    ht = t // 2
    me, c, cx, cy = _where(n)
    o = 1 - c
    p = o * cx + c * cy
    q = o * cy + c * cx
    partner = me + 1 - 2 * c

    def dev(pp, qq):
        return _chip(c, pp, qq) * 2 + c

    pu, pd, qu, qd = dev(p + 1, q), dev(p + 3, q), dev(p, q + 1), dev(p, q + 3)
    _greet([pu, pd, qu, qd, partner])

    loads = []
    for i, (a, b) in enumerate(((w1_ref, w1v), (w3_ref, w3v), (w2_ref, w2v))):
        loads.append(pltpu.make_async_copy(a, b, wsem.at[i]))
    count = [0, 0]

    def bump(i):
        count[i] += 1
        return count[i] - 1

    def copy(b, ref, half, to, sem):
        rows = pl.ds(half * ht, ht)
        return pltpu.make_async_remote_copy(
            src_ref=ref.at[rows], dst_ref=xall.at[b, rows], send_sem=ssem.at[sem], recv_sem=rsem.at[b, half],
            device_id={'expert': to}, device_id_type=MESH)

    def note(b, ref, to, sem):
        return pltpu.make_async_remote_copy(
            src_ref=ref, dst_ref=metas.at[b], send_sem=msem.at[sem], recv_sem=mrsem.at[b],
            device_id={'expert': to}, device_id_type=MESH)

    def send(b, ref, half, to):
        copy(b, ref, half, to, bump(0)).start()

    def tell(b, ref, to):
        note(b, ref, to, bump(1)).start()

    def arrived(b, half):
        copy(b, xall.at[b], half, partner, 0).wait_recv()

    def told(b):
        note(b, metas.at[b], partner, 0).wait_recv()

    for k in (0, 1):
        send(me, x_ref, k, pu)
        send(me, x_ref, 1 - k, pd)
        send(me, x_ref, k, qu)
        send(me, x_ref, 1 - k, qd)
        if k == 0:
            for to in (pu, pd, qu, qd, partner):
                tell(me, meta_ref, to)
    for k in (0, 1):
        send(me, x_ref, k, partner)
    for cp in loads:
        cp.start()
    metas[me] = meta_ref[...]

    def spread(b, half):
        for to in (qu, qd, partner):
            send(b, xall.at[b], half, to)

    def announce(b, first):
        told(b)
        for to in first + (qu, qd, partner):
            tell(b, metas.at[b], to)

    arrived(pd, 0)
    send(pd, xall.at[pd], 0, pu)
    spread(pd, 0)
    arrived(pu, 1)
    send(pu, xall.at[pu], 1, pd)
    spread(pu, 1)
    announce(pd, (pu,))
    announce(pu, ())
    arrived(pd, 1)
    spread(pd, 1)
    arrived(pu, 0)
    spread(pu, 0)
    far = dev(p + 2, q)
    arrived(far, 0)
    spread(far, 0)
    announce(far, ())
    arrived(far, 1)
    spread(far, 1)
    base, mbase = count

    def member(g, i):
        z = ((g + 1) // 2) % 2
        dp = _near(z * (2 * g - 2 + i // 2) + (1 - z) * i)
        dq = z * (1 + 2 * (i % 2)) + (1 - z) * 2 * (g // 3)
        return dp, dq

    def spot(g, i, own):
        dp, dq = member(g, i)
        if own:
            return c, (p + dp) % ND, (q + dq) % ND
        return o, (q + dp) % ND, (p + dq) % ND

    def source(g, i, own):
        k, pp, qq = spot(g, i, own)
        return _chip(k, pp, qq) * 2 + k

    rows = lax.broadcasted_iota(jnp.int32, (r, t), 0)
    nf = f // 3
    dt = d // 4

    def flush(slot):
        for i in range(8):
            pltpu.make_async_copy(hb.at[slot, pl.ds(i * cap, cap)], h_ref.at[0, 0, 0, pl.ds(0, cap)],
                                  osem.at[slot, i]).wait()

    def pass_on(g):
        for i in range(4):
            b = source(g, i, True)
            first = 1 - i % 2
            at = base + ((g - 1) * 4 + i) * 3
            arrived(b, first)
            copy(b, xall.at[b], first, (qd, qu)[i % 2], at).start()
            copy(b, xall.at[b], first, partner, at + 1).start()
            arrived(b, 1 - first)
            copy(b, xall.at[b], 1 - first, partner, at + 2).start()
            told(b)
            mat = mbase + ((g - 1) * 4 + i) * 2
            note(b, metas.at[b], partner, mat).start()
            if i % 2 == 1:
                note(b, metas.at[b], qu, mat + 1).start()

    def finish(g):
        for i in range(4):
            b = source(g, i, True)
            at = base + 24 + i * 2
            arrived(b, 0)
            copy(b, xall.at[b], 0, partner, at).start()
            told(b)
            note(b, metas.at[b], partner, mbase + 16 + i).start()
            arrived(b, 1)
            copy(b, xall.at[b], 1, partner, at + 1).start()

    def group(g, carry):
        pl.when(((g + 1) // 2) % 2 == 1)(lambda: pass_on(g))
        pl.when(g == 3)(lambda: finish(g))
        for i in range(4):
            src = source(g, i, True)
            fetch = pltpu.make_async_copy(xall.at[src], xb.at[i], bsem.at[i])
            if i == 0:
                pl.when(g > 0)(fetch.start)
                pl.when(g == 0)(pltpu.make_async_copy(x_ref, xb.at[0], bsem.at[0]).start)
            else:
                fetch.start()
        for i in range(4):
            src = source(g, i, False)
            arrived(src, 0)
            arrived(src, 1)
            told(src)
            pltpu.make_async_copy(xall.at[src], xb.at[4 + i], bsem.at[4 + i]).start()
        for slot in range(8):
            code = metas[source(g, slot % 4, slot < 4)].astype(jnp.int32) - me * r
            sel = jnp.zeros((r, t), F32)
            for j in range(8):
                sel = sel + jnp.where(rows == code[j:j + 1, :], 1.0, 0.0)
            pltpu.make_async_copy(x_ref, xb.at[slot], bsem.at[slot]).wait()
            xs = jnp.dot(sel.astype(BF16), xb[slot], preferred_element_type=F32).astype(BF16)
            xg[:, slot * cap:(slot + 1) * cap, :] = xs.reshape(el, cap, d)

        def ready():
            for cp in loads:
                cp.wait()
        pl.when(g == 0)(ready)

        def expert(e, carry):
            for m in range(3):
                cols = slice(m * nf, (m + 1) * nf)
                a = jnp.dot(xg[e], w1v[e, :, cols], preferred_element_type=F32)
                b = jnp.dot(xg[e], w3v[e, :, cols], preferred_element_type=F32)
                uv[:, cols] = (a * jax.nn.sigmoid(a) * b).astype(BF16)
            slot = e % 2
            pl.when(g * el + e >= 2)(lambda: flush(slot))
            for m in range(4):
                cols = slice(m * dt, (m + 1) * dt)
                hb[slot, :, cols] = jnp.dot(uv[...], w2v[e, :, cols], preferred_element_type=F32).astype(BF16)
            for i in range(8):
                k, pp, qq = spot(g, i % 4, i < 4)
                pltpu.make_async_copy(hb.at[slot, pl.ds(i * cap, cap)], h_ref.at[k, qq, pp, pl.ds(e * cap, cap)],
                                      osem.at[slot, i]).start()
            return carry
        return lax.fori_loop(0, el, expert, carry)

    lax.fori_loop(0, 4, group, 0)
    flush(0)
    flush(1)

    def sent(i, carry):
        copy(me, x_ref, 0, partner, i).wait_send()
        return carry
    lax.fori_loop(0, base + 32, sent, 0)

    def noted(i, carry):
        note(me, meta_ref, partner, i).wait_send()
        return carry
    lax.fori_loop(0, mbase, noted, 0)
    for i in range(8):
        note(me, meta_ref, partner, mbase + 2 * i).wait_send()
        if i % 2 == 1:
            note(me, meta_ref, partner, mbase + 2 * i + 1).wait_send()
    for i in range(4):
        note(me, meta_ref, partner, mbase + 16 + i).wait_send()


def _return_kernel(n, r, nc, h_ref, meta_ref, y_ref, rx, fwd, acc, r2, r1, gs, gsem, lsem, psem, xsem, fsem,
                   sem2, sem1):
    t, d = y_ref.shape
    dc = d // nc
    me, c, cx, cy = _where(n)
    partner = me + 1 - 2 * c
    ht = t // 2
    frames = ((cx, cy), (cy, cx))
    greet = [partner]
    for k in (0, 1):
        pk, qk = frames[k]
        for s in (1, 3):
            for core in (0, 1):
                greet.append(_chip(k, pk, qk + s) * 2 + core)
    _greet(greet)
    o = 1 - c
    p = o * cx + c * cy
    q = o * cy + c * cx

    def columns(ci):
        return pl.ds(pl.multiple_of(ci * dc, dc), dc)

    def rcopy(src, dst, ssem, rsem, to):
        return pltpu.make_async_remote_copy(src_ref=src, dst_ref=dst, send_sem=ssem, recv_sem=rsem,
                                            device_id={'expert': to}, device_id_type=MESH)

    def rows(k, dq, ci):
        return h_ref.at[k, (frames[k][1] + dq) % ND, :, :, columns(ci)]

    def far(k, dirn, ci):
        pk, qk = frames[k]
        src = h_ref.at[k, (qk + 2) % ND, pl.ds(dirn * 2, 2), :, columns(ci)]
        return rcopy(src, fwd.at[ci, k, dirn], gsem.at[ci, k, dirn], fsem.at[ci, k, dirn],
                     _chip(k, pk, qk + 1 + 2 * dirn) * 2 + c)

    def near(k, dirn, ci):
        pk, qk = frames[k]
        slot = 3 - 2 * dirn
        return rcopy(rows(k, 1 + 2 * dirn, ci), rx.at[ci, slot, c], gsem.at[ci, k, 2 + dirn],
                     xsem.at[ci, slot, c, 0], _chip(k, pk, qk + 1 + 2 * dirn) * 2 + k)

    def other(k, ci):
        return rcopy(rows(k, 0, ci), rx.at[ci, 0, c], gsem.at[ci, k, 4], xsem.at[ci, 0, c, 0], partner)

    def hop(k, dirn, ci):
        pk, qk = frames[k]
        return rcopy(fwd.at[ci, k, dirn], rx.at[ci, 2, c, pl.ds(dirn * 2, 2)], lsem.at[ci, k, dirn],
                     xsem.at[ci, 2, c, dirn], _chip(k, pk, qk + 1 + 2 * dirn) * 2 + k)

    def give(ci):
        for k in (0, 1):
            far(k, 0, ci).start()
            far(k, 1, ci).start()
        for k in (0, 1):
            near(k, 0, ci).start()
            near(k, 1, ci).start()
        for k in (0, 1):
            pl.when(c == k)(pltpu.make_async_copy(rows(k, 0, ci), rx.at[ci, 0, c], xsem.at[ci, 0, c, 0]).start)
            pl.when(c != k)(other(k, ci).start)

    def relay(ci):
        for k in (0, 1):
            for dirn in (0, 1):
                far(k, dirn, ci).wait_recv()
                hop(k, dirn, ci).start()

    def collect(ci):
        for slot in range(4):
            for core in (0, 1):
                if slot == 2:
                    for half in (0, 1):
                        two = pl.ds(half * 2, 2)
                        pltpu.make_async_copy(h_ref.at[0, 0, two, :, columns(0)], rx.at[ci, slot, core, two],
                                              xsem.at[ci, slot, core, half]).wait()
                else:
                    pltpu.make_async_copy(h_ref.at[0, 0, :, :, columns(0)], rx.at[ci, slot, core],
                                          xsem.at[ci, slot, core, 0]).wait()

    lanes = lax.broadcasted_iota(jnp.int32, (t, r), 1)

    def gates(pp, carry):
        src = _chip(c, pp, q) * 2 + c
        meta = meta_ref[src].T
        code = meta[:, :8].astype(jnp.int32)
        for slot in range(4):
            for core in (0, 1):
                base = (_chip(c, p, q + slot) * 2 + core) * r
                gm = jnp.zeros((t, r), F32)
                for i in range(8):
                    gm = gm + jnp.where(code[:, i:i + 1] - base == lanes, meta[:, 8 + i:9 + i], 0.0)
                hi = gm.astype(BF16)
                rest = gm - hi.astype(F32)
                mid = rest.astype(BF16)
                low = (rest - mid.astype(F32)).astype(BF16)
                cols = slice((slot * 2 + core) * r, (slot * 2 + core + 1) * r)
                gs[pp, 0, :, cols] = hi
                gs[pp, 1, :, cols] = mid
                gs[pp, 2, :, cols] = low
        return carry

    def weigh(ci, j, off):
        pp = (p + off) % ND
        rhs = rx[ci, :, :, pp].reshape(8 * r, dc)
        s = jnp.dot(gs[pp, 0], rhs, preferred_element_type=F32)
        s = s + jnp.dot(gs[pp, 1], rhs, preferred_element_type=F32)
        s = s + jnp.dot(gs[pp, 2], rhs, preferred_element_type=F32)
        acc[ci, j] = s

    ends = (_chip(c, p + 1, q) * 2 + c, _chip(c, p + 3, q) * 2 + c)

    def half(i, ci):
        return rcopy(acc.at[ci, 0, pl.ds(i * ht, ht)], r2.at[ci, i], psem.at[ci, i], sem2.at[ci, i], ends[i])

    def whole(i, ci):
        return rcopy(acc.at[ci, 1 + i], r1.at[ci, i], psem.at[ci, 2 + i], sem1.at[ci, i], ends[i])

    def finalize(ci):
        whole(0, ci).wait_recv()
        whole(1, ci).wait_recv()
        y_ref[:, columns(ci)] = (acc[ci, 3] + r1[ci, 0] + r1[ci, 1]).astype(BF16)

    def step(ci, carry):
        pl.when(ci + 1 < nc)(lambda: relay(ci + 1))
        pl.when(ci + 2 < nc)(lambda: give(ci + 2))
        collect(ci)
        weigh(ci, 0, 2)
        half(0, ci).start()
        half(1, ci).start()
        weigh(ci, 1, 1)
        weigh(ci, 2, 3)
        for i in (0, 1):
            half(i, ci).wait_recv()
            own = pl.ds(i * ht, ht)
            acc[ci, 1 + i, own] = acc[ci, 1 + i, own] + r2[ci, i]
            whole(i, ci).start()
        weigh(ci, 3, 0)
        pl.when(ci > 0)(lambda: finalize(ci - 1))
        return carry

    give(0)
    relay(0)
    give(1)
    lax.fori_loop(0, ND, gates, 0)
    lax.fori_loop(0, nc, step, 0)
    finalize(nc - 1)

    def drain(ci, carry):
        for k in (0, 1):
            for dirn in (0, 1):
                far(k, dirn, ci).wait_send()
                near(k, dirn, ci).wait_send()
                hop(k, dirn, ci).wait_send()
            pl.when(c != k)(other(k, ci).wait_send)
        for i in (0, 1):
            half(i, ci).wait_send()
            whole(i, ci).wait_send()
        return carry
    lax.fori_loop(0, nc, drain, 0)


def solution(mesh):
    n = mesh.shape['expert']
    assert n == 2 * ND * ND

    def local(x, idx, g, hot_tok, w1, w3, w2):
        t, d = x.shape
        k = idx.shape[1]
        el, _, f = w1.shape
        e = el * n
        ch = hot_tok.shape[0]
        cap = max(ch, 2 * ((t * k - ch + e - 2) // (e - 1)))
        r = el * cap
        nc = 4
        dc = d // nc

        hit = idx[:, :, None] == jnp.arange(e, dtype=jnp.int32)
        chosen = hit.any(axis=1).astype(BF16)
        earlier = (jnp.arange(t)[:, None] > jnp.arange(t)[None, :]).astype(BF16)
        before = jnp.dot(earlier, chosen, preferred_element_type=F32)
        rank = jnp.where(hit, before[:, None, :], 0.0).sum(axis=2)
        code = (idx * cap).astype(F32) + rank
        meta = jnp.concatenate([code.T, g.T], axis=0)

        anyspec = pl.BlockSpec(memory_space=pl.ANY)
        vspec = pl.BlockSpec(memory_space=pltpu.VMEM)
        h, _, metas = pl.pallas_call(
            functools.partial(_dispatch_kernel, n, el, cap),
            out_shape=[jax.ShapeDtypeStruct((2, ND, ND, r, d), BF16), jax.ShapeDtypeStruct((n, t, d), BF16),
                       jax.ShapeDtypeStruct((n,) + meta.shape, F32)],
            in_specs=[anyspec, vspec, anyspec, anyspec, anyspec],
            out_specs=[anyspec, anyspec, vspec],
            scratch_shapes=[
                pltpu.VMEM(w1.shape, BF16), pltpu.VMEM(w3.shape, BF16), pltpu.VMEM(w2.shape, BF16),
                pltpu.VMEM((8, t, d), BF16), pltpu.VMEM((el, 8 * cap, d), BF16),
                pltpu.VMEM((8 * cap, f), BF16), pltpu.VMEM((2, 8 * cap, d), BF16),
                pltpu.SemaphoreType.DMA((3,)), pltpu.SemaphoreType.DMA((8,)), pltpu.SemaphoreType.DMA((2, 8)),
                pltpu.SemaphoreType.DMA((62,)), pltpu.SemaphoreType.DMA((n, 2)),
                pltpu.SemaphoreType.DMA((35,)), pltpu.SemaphoreType.DMA((n,)),
            ],
            compiler_params=pltpu.CompilerParams(collective_id=0, has_side_effects=True,
                                                 vmem_limit_bytes=66_000_000),
        )(x, meta, w1, w3, w2)
        return pl.pallas_call(
            functools.partial(_return_kernel, n, r, nc),
            out_shape=jax.ShapeDtypeStruct((t, d), BF16),
            in_specs=[anyspec, vspec],
            out_specs=vspec,
            scratch_shapes=[
                pltpu.VMEM((nc, 4, 2, ND, r, dc), BF16), pltpu.VMEM((nc, 2, 2, 2, r, dc), BF16),
                pltpu.VMEM((nc, 4, t, dc), F32), pltpu.VMEM((nc, 2, t // 2, dc), F32),
                pltpu.VMEM((nc, 2, t, dc), F32), pltpu.VMEM((ND, 3, t, 8 * r), BF16),
                pltpu.SemaphoreType.DMA((nc, 2, 5)), pltpu.SemaphoreType.DMA((nc, 2, 2)),
                pltpu.SemaphoreType.DMA((nc, 4)), pltpu.SemaphoreType.DMA((nc, 4, 2, 2)),
                pltpu.SemaphoreType.DMA((nc, 2, 2)), pltpu.SemaphoreType.DMA((nc, 2)),
                pltpu.SemaphoreType.DMA((nc, 2)),
            ],
            compiler_params=pltpu.CompilerParams(collective_id=1, has_side_effects=True,
                                                 vmem_limit_bytes=60_000_000),
        )(h, metas)

    rows = P(('data', 'expert'))
    wspec = P('expert')
    return jax.shard_map(local, mesh=mesh, in_specs=(rows, rows, rows, rows, wspec, wspec, wspec), out_specs=rows,
                         check_vma=False)
```

time: 695 us -> 281 us (0.40)
  the two profiles are of different devices: /device:TPU:107 before, /device:TPU:97 now
where the time goes in v2:
time: 281 us; the launch traced here: 280 us
  Pallas kernels  273 us (97%)
  other arithmetic  3.35 us (1%)
  local copies, waits for them, and re-layouts  3.18 us (1%)
    pallas_call x1, Pallas kernels, local(): pl.pallas_call(functools.partial(_return_kernel, n, r, nc), out_shape=jax...  141 us
    pallas_call x1, Pallas kernels, local(): pl.pallas_call(functools.partial(_dispatch_kernel, n, el, cap), out_shape...  133 us

profile of v2, /device:TPU:97, one launch (start us, length us, event | category | flops | bytes accessed | tf_op | source)
XLA Modules:
  0.0 280.2 jit_solution(12443510294982826053)
XLA Ops:
  0.0 0.8 copy.8
  0.8 0.4 fusion
  1.3 0.2 fusion.1
  1.5 0.9 select_reduce_fusion
  2.3 0.1 copy.9
  2.4 0.7 add_bitcast_fusion
  3.1 1.3 pad_maximum_fusion.meta_ref
  4.4 132.8 %shard_map.64 = (bf16[2,4,4,128,2048]{4,3,2,1,0:T(8,128)(2,1)}, bf16[32,256,2048]{2,1,0:T(8,128)(2,1)}, f32[32,16,256]{2,1,0:T(8,128)}) custom-call(bf16[256,2048]{1,0:T(8,128)(2,1)} %x_ref.1, f32[16,256]{1,0:T(8,128)} %pad_maximum_fusion.meta_ref, bf16[4,2048,768]{2,1,0:T(8,128)(2,1)} %w1_ref.1, bf16[4,2048,768]{2,1,0:T(8,128)(2,1)} %w3_ref.1, ...), custom_call_target="tpu_custom_call" | custom-call | tf_op jit(solution)/shard_map/pallas_call | solution.py:441
  137.2 140.7 %shard_map.65 = bf16[256,2048]{1,0:T(8,128)(2,1)} custom-call(bf16[2,4,4,128,2048]{4,3,2,1,0:T(8,128)(2,1)} %get-tuple-element.7.h_ref, f32[32,16,256]{2,1,0:T(8,128)} %get-tuple-element.8.meta_ref), custom_call_target="tpu_custom_call" | custom-call | tf_op jit(solution)/shard_map/pallas_call | solution.py:458
  277.9 2.3 copy.11

commit v3 on v2

v3 whole, which is shorter than its diff:
```python
import functools
import math

import jax
import jax.numpy as jnp
from jax import lax
from jax.experimental import pallas as pl
from jax.experimental.pallas import tpu as pltpu
from jax.sharding import PartitionSpec as P

MESH = pl.DeviceIdType.MESH
F32 = jnp.float32
BF16 = jnp.bfloat16
ND = 4


def _where(n):
    me = lax.axis_index('expert')
    c = me % 2
    chip = me // 2
    return me, c, chip % ND, chip // ND


def _chip(k, p, q):
    p = p % ND
    q = q % ND
    return (1 - k) * (q * ND + p) + k * (p * ND + q)


def _around(frames):
    return [_chip(k, frames[k][0], frames[k][1] + s) * 2 + core for k in (0, 1) for s in (1, 3) for core in (0, 1)]


def _greet(devs):
    bar = pltpu.get_barrier_semaphore()
    for dev in devs:
        pl.semaphore_signal(bar, inc=1, device_id={'expert': dev}, device_id_type=MESH)
    pl.semaphore_wait(bar, len(devs))


def _dispatch_kernel(n, el, cap, nc, x_ref, meta_ref, w1_ref, w3_ref, w2_ref, *refs):
    h_refs, (xall, metas, rn), refs = refs[:nc], refs[nc:nc + 3], refs[nc + 3:]
    hbs, (w1v, w3v, w2v, xb, xg, uv, wsem, bsem, osem, ssem, rsem, msem, mrsem,
          nsem, nrsem) = refs[:nc], refs[nc:]
    t, d = x_ref.shape
    f = w1v.shape[2]
    r = el * cap
    ht = t // 2
    me, c, cx, cy = _where(n)
    o = 1 - c
    p = o * cx + c * cy
    q = o * cy + c * cx
    partner = me + 1 - 2 * c

    def dev(pp, qq):
        return _chip(c, pp, qq) * 2 + c

    pu, pd, qu, qd = dev(p + 1, q), dev(p + 3, q), dev(p, q + 1), dev(p, q + 3)
    frames = ((cx, cy), (cy, cx))
    _greet(_around(frames) + [partner])

    loads = []
    for i, (a, b) in enumerate(((w1_ref, w1v), (w3_ref, w3v), (w2_ref, w2v))):
        loads.append(pltpu.make_async_copy(a, b, wsem.at[i]))
    count = [0, 0]

    def bump(i):
        count[i] += 1
        return count[i] - 1

    def copy(b, ref, half, to, sem):
        rows = pl.ds(0, t) if half is None else pl.ds(half * ht, ht)
        half = half or 0
        return pltpu.make_async_remote_copy(
            src_ref=ref.at[rows], dst_ref=xall.at[b, rows], send_sem=ssem.at[sem], recv_sem=rsem.at[b, half],
            device_id={'expert': to}, device_id_type=MESH)

    def note(b, ref, to, sem):
        return pltpu.make_async_remote_copy(
            src_ref=ref, dst_ref=metas.at[b], send_sem=msem.at[sem], recv_sem=mrsem.at[b],
            device_id={'expert': to}, device_id_type=MESH)

    sizes = []

    def send(b, ref, half, to):
        sizes.append(half)
        copy(b, ref, half, to, bump(0)).start()

    def tell(b, ref, to):
        note(b, ref, to, bump(1)).start()

    def arrived(b, half):
        copy(b, xall.at[b], half, partner, 0).wait_recv()

    def told(b):
        note(b, metas.at[b], partner, 0).wait_recv()

    for k in (0, 1):
        send(me, x_ref, k, pu)
        send(me, x_ref, 1 - k, pd)
        send(me, x_ref, k, qu)
        send(me, x_ref, 1 - k, qd)
        if k == 0:
            for to in (pu, pd, qu, qd, partner):
                tell(me, meta_ref, to)
    send(me, x_ref, None, partner)
    for cp in loads:
        cp.start()
    metas[me] = meta_ref[...]

    def spread(b):
        for to in (qu, qd, partner):
            send(b, xall.at[b], None, to)

    def announce(b, *to):
        told(b)
        for to in to:
            tell(b, metas.at[b], to)

    def ring():
        arrived(pd, 0)
        send(pd, xall.at[pd], 0, pu)
        arrived(pu, 1)
        send(pu, xall.at[pu], 1, pd)
        announce(pd, pu, qu, qd, partner)
        announce(pu, qu, qd, partner)
        arrived(pd, 1)
        spread(pd)
        arrived(pu, 0)
        spread(pu)

    def take(dp, dq):
        b = dev(p + dp, q + dq)
        first = 1 if dq == 1 else 0
        on = qd if dq == 1 else qu
        if dq in (1, 3) and dp:
            arrived(b, None)
            send(b, xall.at[b], first, on)
        else:
            arrived(b, first)
            if dq in (1, 3):
                send(b, xall.at[b], first, on)
            arrived(b, 1 - first)
        if dq == 0:
            spread(b)
            announce(b, qu, qd, partner)
            return
        send(b, xall.at[b], None, partner)
        if dq == 3:
            announce(b, qu, partner)
        else:
            announce(b, partner)

    def spot(dp, dq, own):
        if own:
            return c, (p + dp) % ND, (q + dq) % ND
        return o, (q + dp) % ND, (p + dq) % ND

    def source(dp, dq, own):
        k, pp, qq = spot(dp, dq, own)
        return _chip(k, pp, qq) * 2 + k

    rows = lax.broadcasted_iota(jnp.int32, (r, t), 0)
    nf = f // 3
    dt = math.gcd(512, *(hb.shape[-1] for hb in hbs))

    def flush(slot, m):
        for i in range(m):
            for j in range(nc):
                pltpu.make_async_copy(hbs[j].at[slot, pl.ds(i * cap, cap)], h_refs[j].at[0, 0, 0, pl.ds(0, cap)],
                                      osem.at[slot, i, j]).wait()

    def fetch(slot, dp, dq, own):
        src = source(dp, dq, own)
        ref = x_ref if own and dp == 0 and dq == 0 else xall.at[src]
        pltpu.make_async_copy(ref, xb.at[slot], bsem.at[slot]).start()

    def select(slot, dp, dq, own):
        code = metas[source(dp, dq, own)].astype(jnp.int32) - me * r
        hit = rows == code[0:1, :]
        for j in range(1, 8):
            hit = hit | (rows == code[j:j + 1, :])
        sel = jnp.where(hit, 1.0, 0.0).astype(BF16)
        pltpu.make_async_copy(x_ref, xb.at[slot], bsem.at[slot]).wait()
        xs = jnp.dot(sel, xb[slot], preferred_element_type=F32).astype(BF16)
        xg[:, slot * cap:(slot + 1) * cap, :] = xs.reshape(el, cap, d)

    def group(members, before, first=False):
        nb = len(members)
        m = 2 * nb * cap
        for i, (dp, dq) in enumerate(members):
            fetch(i, dp, dq, True)
        for i, (dp, dq) in enumerate(members):
            select(i, dp, dq, True)
        for i, (dp, dq) in enumerate(members):
            src = source(dp, dq, False)
            arrived(src, None)
            told(src)
            fetch(nb + i, dp, dq, False)
        for i, (dp, dq) in enumerate(members):
            select(nb + i, dp, dq, False)
        if first:
            for cp in loads:
                cp.wait()

        def expert(e, carry):
            for i in range(3):
                cols = slice(i * nf, (i + 1) * nf)
                a = jnp.dot(xg[e, 0:m], w1v[e, :, cols], preferred_element_type=F32)
                b = jnp.dot(xg[e, 0:m], w3v[e, :, cols], preferred_element_type=F32)
                uv[0:m, cols] = (a * jax.nn.sigmoid(a) * b).astype(BF16)
            slot = e % 2
            if before == 2 * nb:
                flush(slot, before)
            else:
                pl.when(e >= 2)(lambda: flush(slot, 2 * nb))
                if before:
                    pl.when(e < 2)(lambda: flush(slot, before))
            at = 0
            for hb in hbs:
                for i in range(0, hb.shape[-1], dt):
                    hb[slot, 0:m, i:i + dt] = jnp.dot(uv[0:m], w2v[e, :, at:at + dt],
                                                      preferred_element_type=F32).astype(BF16)
                    at += dt
            for i in range(2 * nb):
                k, pp, qq = spot(*members[i % nb], i < nb)
                for j in range(nc):
                    pltpu.make_async_copy(hbs[j].at[slot, pl.ds(i * cap, cap)],
                                          h_refs[j].at[k, qq, pp, pl.ds(e * cap, cap)], osem.at[slot, i, j]).start()
            return carry
        lax.fori_loop(0, el, expert, 0)
        return 2 * nb

    ring()
    take(0, 1)
    take(0, 3)
    done = group(((0, 0), (1, 0), (3, 0), (0, 1)), 0, True)
    take(2, 0)
    take(3, 1)
    take(3, 3)
    done = group(((0, 3), (2, 0), (3, 1), (3, 3)), done)
    take(1, 1)
    take(1, 3)
    take(2, 1)
    take(2, 3)
    done = group(((1, 1), (1, 3), (2, 1), (2, 3)), done)
    flush(0, done)
    flush(1, done)
    ahead = []
    for k in (0, 1):
        pk, qk = frames[k]
        for dirn, s in ((0, 1), (1, 3)):
            ahead.append(pltpu.make_async_remote_copy(
                src_ref=h_refs[0].at[k, (qk + s) % ND], dst_ref=rn.at[dirn, c], send_sem=nsem.at[k, dirn],
                recv_sem=nrsem.at[dirn, c], device_id={'expert': _chip(k, pk, qk + s) * 2 + k}, device_id_type=MESH))
    for cp in ahead:
        cp.start()
    take(0, 2)
    take(3, 2)
    done = group(((0, 2), (3, 2)), 0)
    take(1, 2)
    take(2, 2)
    done = group(((1, 2), (2, 2)), done)
    flush(0, done)
    flush(1, done)

    for i, half in enumerate(sizes):
        copy(me, x_ref, half, partner, i).wait_send()

    for cp in ahead:
        cp.wait_send()
    for dirn in (0, 1):
        for core in (0, 1):
            pltpu.make_async_remote_copy(
                src_ref=rn.at[dirn, core], dst_ref=rn.at[dirn, core], send_sem=nsem.at[0, 0],
                recv_sem=nrsem.at[dirn, core], device_id={'expert': partner}, device_id_type=MESH).wait_recv()

    def noted(i, carry):
        note(me, meta_ref, partner, i).wait_send()
        return carry
    lax.fori_loop(0, count[1], noted, 0)
    assert count == [40, 31]


def _return_kernel(n, r, nc, *refs):
    h_refs, (meta_ref, rn, y_ref), refs = refs[:nc], refs[nc:nc + 3], refs[nc + 3:]
    rx, fwd, acc, r2, r1 = (refs[i * nc:(i + 1) * nc] for i in range(5))
    gs, gsem, lsem, psem, xsem, fsem, sem2, sem1 = refs[5 * nc:]
    t, d = y_ref.shape
    widths = [h.shape[-1] for h in h_refs]
    starts = [sum(widths[:i]) for i in range(nc)]
    me, c, cx, cy = _where(n)
    partner = me + 1 - 2 * c
    ht = t // 2
    frames = ((cx, cy), (cy, cx))
    _greet(_around(frames) + [partner])
    o = 1 - c
    p = o * cx + c * cy
    q = o * cy + c * cx

    def rcopy(src, dst, ssem, rsem, to):
        return pltpu.make_async_remote_copy(src_ref=src, dst_ref=dst, send_sem=ssem, recv_sem=rsem,
                                            device_id={'expert': to}, device_id_type=MESH)

    def rows(k, dq, ci):
        return h_refs[ci].at[k, (frames[k][1] + dq) % ND]

    def far(k, dirn, ci):
        pk, qk = frames[k]
        src = h_refs[ci].at[k, (qk + 2) % ND, pl.ds(dirn * 2, 2)]
        return rcopy(src, fwd[ci].at[k, dirn], gsem.at[ci, k, dirn], fsem.at[ci, k, dirn],
                     _chip(k, pk, qk + 1 + 2 * dirn) * 2 + c)

    def near(k, dirn, ci):
        pk, qk = frames[k]
        slot = 3 - 2 * dirn
        return rcopy(rows(k, 1 + 2 * dirn, ci), rx[ci].at[slot, c], gsem.at[ci, k, 2 + dirn],
                     xsem.at[ci, slot, c, 0], _chip(k, pk, qk + 1 + 2 * dirn) * 2 + k)

    def other(k, ci):
        return rcopy(rows(k, 0, ci), rx[ci].at[0, c], gsem.at[ci, k, 4], xsem.at[ci, 0, c, 0], partner)

    def hop(k, dirn, ci):
        pk, qk = frames[k]
        return rcopy(fwd[ci].at[k, dirn], rx[ci].at[2, c, pl.ds(dirn * 2, 2)], lsem.at[ci, k, dirn],
                     xsem.at[ci, 2, c, dirn], _chip(k, pk, qk + 1 + 2 * dirn) * 2 + k)

    def give(ci):
        for k in (0, 1):
            far(k, 0, ci).start()
            far(k, 1, ci).start()
        for k in (0, 1):
            for dirn in (0, 1):
                if ci:
                    near(k, dirn, ci).start()
                else:
                    slot = 3 - 2 * dirn
                    pltpu.make_async_copy(rn.at[dirn, k], rx[0].at[slot, k], xsem.at[0, slot, k, 0]).start()
        for k in (0, 1):
            pl.when(c == k)(pltpu.make_async_copy(rows(k, 0, ci), rx[ci].at[0, c], xsem.at[ci, 0, c, 0]).start)
            pl.when(c != k)(other(k, ci).start)

    def relay(ci):
        for k in (0, 1):
            for dirn in (0, 1):
                far(k, dirn, ci).wait_recv()
                hop(k, dirn, ci).start()

    def collect(ci):
        for slot in range(4):
            for core in (0, 1):
                if slot == 2:
                    for half in (0, 1):
                        two = pl.ds(half * 2, 2)
                        pltpu.make_async_copy(h_refs[ci].at[0, 0, two], rx[ci].at[slot, core, two],
                                              xsem.at[ci, slot, core, half]).wait()
                else:
                    pltpu.make_async_copy(h_refs[ci].at[0, 0], rx[ci].at[slot, core],
                                          xsem.at[ci, slot, core, 0]).wait()

    lanes = lax.broadcasted_iota(jnp.int32, (t, r), 1)

    def gates(pp, carry):
        src = _chip(c, pp, q) * 2 + c
        meta = meta_ref[src].T
        code = meta[:, :8].astype(jnp.int32)
        for slot in range(4):
            for core in (0, 1):
                base = (_chip(c, p, q + slot) * 2 + core) * r
                gm = jnp.zeros((t, r), F32)
                for i in range(8):
                    gm = gm + jnp.where(code[:, i:i + 1] - base == lanes, meta[:, 8 + i:9 + i], 0.0)
                hi = gm.astype(BF16)
                rest = gm - hi.astype(F32)
                mid = rest.astype(BF16)
                low = (rest - mid.astype(F32)).astype(BF16)
                cols = slice((slot * 2 + core) * r, (slot * 2 + core + 1) * r)
                gs[pp, 0, :, cols] = hi
                gs[pp, 1, :, cols] = mid
                gs[pp, 2, :, cols] = low
        return carry

    def weigh(ci, j, off):
        pp = (p + off) % ND
        w = math.gcd(512, widths[ci])

        def tile(i, carry):
            cols = pl.ds(pl.multiple_of(i * w, w), w)
            rhs = rx[ci][:, :, pp, :, cols].reshape(8 * r, w)
            s = jnp.dot(gs[pp, 0], rhs, preferred_element_type=F32)
            s = s + jnp.dot(gs[pp, 1], rhs, preferred_element_type=F32)
            s = s + jnp.dot(gs[pp, 2], rhs, preferred_element_type=F32)
            acc[ci][j, :, cols] = s
            return carry
        lax.fori_loop(0, widths[ci] // w, tile, 0)

    ends = (_chip(c, p + 1, q) * 2 + c, _chip(c, p + 3, q) * 2 + c)

    def half(i, ci):
        return rcopy(acc[ci].at[0, pl.ds(i * ht, ht)], r2[ci].at[i], psem.at[ci, i], sem2.at[ci, i], ends[i])

    def whole(i, ci):
        return rcopy(acc[ci].at[1 + i], r1[ci].at[i], psem.at[ci, 2 + i], sem1.at[ci, i], ends[i])

    def finalize(ci):
        whole(0, ci).wait_recv()
        whole(1, ci).wait_recv()
        y_ref[:, starts[ci]:starts[ci] + widths[ci]] = (acc[ci][3] + r1[ci][0] + r1[ci][1]).astype(BF16)

    give(0)
    relay(0)
    give(1)
    lax.fori_loop(0, ND, gates, 0)
    for ci in range(nc):
        if ci + 1 < nc:
            relay(ci + 1)
        if ci + 2 < nc:
            give(ci + 2)
        collect(ci)
        weigh(ci, 0, 2)
        half(0, ci).start()
        half(1, ci).start()
        weigh(ci, 1, 1)
        weigh(ci, 2, 3)
        for i in (0, 1):
            half(i, ci).wait_recv()
            own = pl.ds(i * ht, ht)
            acc[ci][1 + i, own] = acc[ci][1 + i, own] + r2[ci][i]
            whole(i, ci).start()
        weigh(ci, 3, 0)
        if ci:
            finalize(ci - 1)
    finalize(nc - 1)
    for ci in range(nc):
        for k in (0, 1):
            for dirn in (0, 1):
                far(k, dirn, ci).wait_send()
                if ci:
                    near(k, dirn, ci).wait_send()
                hop(k, dirn, ci).wait_send()
            pl.when(c != k)(other(k, ci).wait_send)
        for i in (0, 1):
            half(i, ci).wait_send()
            whole(i, ci).wait_send()


def solution(mesh):
    n = mesh.shape['expert']
    assert n == 2 * ND * ND

    def local(x, idx, g, hot_tok, w1, w3, w2):
        t, d = x.shape
        k = idx.shape[1]
        el, _, f = w1.shape
        e = el * n
        ch = hot_tok.shape[0]
        cap = max(ch, 2 * ((t * k - ch + e - 2) // (e - 1)))
        r = el * cap
        widths = [d * i // 16 for i in (8, 8)]
        nc = len(widths)

        hit = idx[:, :, None] == jnp.arange(e, dtype=jnp.int32)
        chosen = hit.any(axis=1).astype(BF16)
        earlier = (jnp.arange(t)[:, None] > jnp.arange(t)[None, :]).astype(BF16)
        before = jnp.dot(earlier, chosen, preferred_element_type=F32)
        rank = jnp.where(hit, before[:, None, :], 0.0).sum(axis=2)
        code = (idx * cap).astype(F32) + rank
        meta = jnp.concatenate([code.T, g.T], axis=0)

        anyspec = pl.BlockSpec(memory_space=pl.ANY)
        vspec = pl.BlockSpec(memory_space=pltpu.VMEM)
        *h, _, metas, near = pl.pallas_call(
            functools.partial(_dispatch_kernel, n, el, cap, nc),
            out_shape=[jax.ShapeDtypeStruct((2, ND, ND, r, w), BF16) for w in widths]
            + [jax.ShapeDtypeStruct((n, t, d), BF16),
               jax.ShapeDtypeStruct((n,) + meta.shape, F32),
               jax.ShapeDtypeStruct((2, 2, ND, r, widths[0]), BF16)],
            in_specs=[anyspec, vspec, anyspec, anyspec, anyspec],
            out_specs=[anyspec] * (nc + 1) + [vspec, anyspec],
            scratch_shapes=[pltpu.VMEM((2, 8 * cap, w), BF16) for w in widths] + [
                pltpu.VMEM(w1.shape, BF16), pltpu.VMEM(w3.shape, BF16), pltpu.VMEM(w2.shape, BF16),
                pltpu.VMEM((8, t, d), BF16), pltpu.VMEM((el, 8 * cap, d), BF16),
                pltpu.VMEM((8 * cap, f), BF16),
                pltpu.SemaphoreType.DMA((3,)), pltpu.SemaphoreType.DMA((8,)), pltpu.SemaphoreType.DMA((2, 8, nc)),
                pltpu.SemaphoreType.DMA((40,)), pltpu.SemaphoreType.DMA((n, 2)),
                pltpu.SemaphoreType.DMA((31,)), pltpu.SemaphoreType.DMA((n,)),
                pltpu.SemaphoreType.DMA((2, 2)), pltpu.SemaphoreType.DMA((2, 2)),
            ],
            compiler_params=pltpu.CompilerParams(collective_id=0, has_side_effects=True,
                                                 vmem_limit_bytes=66_000_000),
        )(x, meta, w1, w3, w2)
        return pl.pallas_call(
            functools.partial(_return_kernel, n, r, nc),
            out_shape=jax.ShapeDtypeStruct((t, d), BF16),
            in_specs=[anyspec] * nc + [vspec, anyspec],
            out_specs=vspec,
            scratch_shapes=[pltpu.VMEM((4, 2, ND, r, w), BF16) for w in widths]
            + [pltpu.VMEM((2, 2, 2, r, w), BF16) for w in widths]
            + [pltpu.VMEM((4, t, w), F32) for w in widths]
            + [pltpu.VMEM((2, t // 2, w), F32) for w in widths]
            + [pltpu.VMEM((2, t, w), F32) for w in widths] + [
                pltpu.VMEM((ND, 3, t, 8 * r), BF16),
                pltpu.SemaphoreType.DMA((nc, 2, 5)), pltpu.SemaphoreType.DMA((nc, 2, 2)),
                pltpu.SemaphoreType.DMA((nc, 4)), pltpu.SemaphoreType.DMA((nc, 4, 2, 2)),
                pltpu.SemaphoreType.DMA((nc, 2, 2)), pltpu.SemaphoreType.DMA((nc, 2)),
                pltpu.SemaphoreType.DMA((nc, 2)),
            ],
            compiler_params=pltpu.CompilerParams(collective_id=1, has_side_effects=True,
                                                 vmem_limit_bytes=60_000_000),
        )(*h, metas, near)

    rows = P(('data', 'expert'))
    wspec = P('expert')
    return jax.shard_map(local, mesh=mesh, in_specs=(rows, rows, rows, rows, wspec, wspec, wspec), out_specs=rows,
                         check_vma=False)
```

time: 281 us -> 246 us (0.88)
  Pallas kernels: 273 us -> 239 us
    pallas_call x1, Pallas kernels: 141 us -> 114 us  [local(): pl.pallas_call(functools.partial(_return_kernel, n, r, nc), out_shape=jax...]
    pallas_call x1, Pallas kernels: 133 us -> 125 us  [local(): pl.pallas_call(functools.partial(_dispatch_kernel, n, el, cap, nc), out_s...]
where the time goes in v3:
time: 246 us
  Pallas kernels  239 us (97%)
  other arithmetic  3.35 us (1%)
  local copies, waits for them, and re-layouts  3.18 us (1%)
    pallas_call x1, Pallas kernels, local(): pl.pallas_call(functools.partial(_dispatch_kernel, n, el, cap, nc), out_s...  125 us
    pallas_call x1, Pallas kernels, local(): pl.pallas_call(functools.partial(_return_kernel, n, r, nc), out_shape=jax...  114 us

profile of v3, /device:TPU:97, one launch (start us, length us, event | category | flops | bytes accessed | tf_op | source)
XLA Modules:
  0.0 245.8 jit_solution(11646491684511693648)
XLA Ops:
  0.0 0.8 copy.8
  0.8 0.4 fusion
  1.3 0.2 fusion.1
  1.5 0.9 select_reduce_fusion
  2.3 0.1 copy.9
  2.4 0.7 add_bitcast_fusion
  3.1 1.3 pad_maximum_fusion.meta_ref
  4.4 124.9 %shard_map.64 = (bf16[2,4,4,128,1024]{4,3,2,1,0:T(8,128)(2,1)}, bf16[2,4,4,128,1024]{4,3,2,1,0:T(8,128)(2,1)}, bf16[32,256,2048]{2,1,0:T(8,128)(2,1)}, f32[32,16...) custom-call(bf16[256,2048]{1,0:T(8,128)(2,1)} %x_ref.1, f32[16,256]{1,0:T(8,128)} %pad_maximum_fusion.meta_ref, ...), custom_call_target="tpu_custom_call" | custom-call | tf_op jit(solution)/shard_map/pallas_call | solution.py:472
  129.4 114.1 %shard_map.65 = bf16[256,2048]{1,0:T(8,128)(2,1)} custom-call(bf16[2,4,4,128,1024]{4,3,2,1,0:T(8,128)(2,1)} %get-tuple-element.9.refs_0_, bf16[2,4,4,128,1024]{4,3,2,1,0:T(8,128)(2,1)} %get-tuple-element.10.refs_1_, f32[32,16,256]{2,1,0:T(8,128)} %get-tuple-element.11.refs_2_, bf16[2,2,4,128,1024]{4,3,2,1,0:T(8,128)(2,1)} %get-tuple-element.12.refs_3_), custom_call_target="tpu_custom_call" | custom-call | tf_op jit(solution)/shard_map/pallas_call | solution.py:492
  243.5 2.3 copy.11

commit v4 on v3

--- a/solution.py
+++ b/solution.py
@@ -38,7 +38,7 @@
     pl.semaphore_wait(bar, len(devs))
 
 
-def _dispatch_kernel(n, el, cap, nc, x_ref, meta_ref, w1_ref, w3_ref, w2_ref, *refs):
+def _dispatch_kernel(n, el, cap, nc, x_ref, idx_ref, g_ref, w1_ref, w3_ref, w2_ref, *refs):
     h_refs, (xall, metas, rn), refs = refs[:nc], refs[nc:nc + 3], refs[nc + 3:]
     hbs, (w1v, w3v, w2v, xb, xg, uv, wsem, bsem, osem, ssem, rsem, msem, mrsem,
           nsem, nrsem) = refs[:nc], refs[nc:]
@@ -95,18 +95,36 @@
     def told(b):
         note(b, metas.at[b], partner, 0).wait_recv()
 
+    def take_notes():
+        top = idx_ref.shape[0]
+        ids = idx_ref[...]
+        experts = lax.broadcasted_iota(jnp.int32, (n * el, t), 0)
+        hit = experts == ids[0:1, :]
+        for j in range(1, top):
+            hit = hit | (experts == ids[j:j + 1, :])
+        chosen = jnp.where(hit, 1.0, 0.0).astype(BF16)
+        earlier = lax.broadcasted_iota(jnp.int32, (t, t), 0) < lax.broadcasted_iota(jnp.int32, (t, t), 1)
+        before = jnp.dot(chosen, jnp.where(earlier, 1.0, 0.0).astype(BF16), preferred_element_type=F32)
+        row = lax.broadcasted_iota(jnp.int32, (top, t), 0)
+        place = ids.astype(F32) * cap
+        for j in range(top):
+            rank = jnp.sum(jnp.where(experts == ids[j:j + 1, :], before, 0.0), axis=0, keepdims=True)
+            place = place + jnp.where(row == j, rank, 0.0)
+        metas[me, 0:top] = place
+        metas[me, top:2 * top] = g_ref[...]
+
     for k in (0, 1):
         send(me, x_ref, k, pu)
         send(me, x_ref, 1 - k, pd)
         send(me, x_ref, k, qu)
         send(me, x_ref, 1 - k, qd)
         if k == 0:
+            take_notes()
             for to in (pu, pd, qu, qd, partner):
-                tell(me, meta_ref, to)
+                tell(me, metas.at[me], to)
     send(me, x_ref, None, partner)
     for cp in loads:
         cp.start()
-    metas[me] = meta_ref[...]
 
     def spread(b):
         for to in (qu, qd, partner):
@@ -276,7 +294,7 @@
                 recv_sem=nrsem.at[dirn, core], device_id={'expert': partner}, device_id_type=MESH).wait_recv()
 
     def noted(i, carry):
-        note(me, meta_ref, partner, i).wait_send()
+        note(me, metas.at[me], partner, i).wait_send()
         return carry
     lax.fori_loop(0, count[1], noted, 0)
     assert count == [40, 31]
@@ -459,23 +477,15 @@
         widths = [d * i // 16 for i in (8, 8)]
         nc = len(widths)
 
-        hit = idx[:, :, None] == jnp.arange(e, dtype=jnp.int32)
-        chosen = hit.any(axis=1).astype(BF16)
-        earlier = (jnp.arange(t)[:, None] > jnp.arange(t)[None, :]).astype(BF16)
-        before = jnp.dot(earlier, chosen, preferred_element_type=F32)
-        rank = jnp.where(hit, before[:, None, :], 0.0).sum(axis=2)
-        code = (idx * cap).astype(F32) + rank
-        meta = jnp.concatenate([code.T, g.T], axis=0)
-
         anyspec = pl.BlockSpec(memory_space=pl.ANY)
         vspec = pl.BlockSpec(memory_space=pltpu.VMEM)
         *h, _, metas, near = pl.pallas_call(
             functools.partial(_dispatch_kernel, n, el, cap, nc),
             out_shape=[jax.ShapeDtypeStruct((2, ND, ND, r, w), BF16) for w in widths]
             + [jax.ShapeDtypeStruct((n, t, d), BF16),
-               jax.ShapeDtypeStruct((n,) + meta.shape, F32),
+               jax.ShapeDtypeStruct((n, 2 * k, t), F32),
                jax.ShapeDtypeStruct((2, 2, ND, r, widths[0]), BF16)],
-            in_specs=[anyspec, vspec, anyspec, anyspec, anyspec],
+            in_specs=[anyspec, vspec, vspec, anyspec, anyspec, anyspec],
             out_specs=[anyspec] * (nc + 1) + [vspec, anyspec],
             scratch_shapes=[pltpu.VMEM((2, 8 * cap, w), BF16) for w in widths] + [
                 pltpu.VMEM(w1.shape, BF16), pltpu.VMEM(w3.shape, BF16), pltpu.VMEM(w2.shape, BF16),
@@ -488,7 +498,7 @@
             ],
             compiler_params=pltpu.CompilerParams(collective_id=0, has_side_effects=True,
                                                  vmem_limit_bytes=66_000_000),
-        )(x, meta, w1, w3, w2)
+        )(x, idx.T, g.T, w1, w3, w2)
         return pl.pallas_call(
             functools.partial(_return_kernel, n, r, nc),
             out_shape=jax.ShapeDtypeStruct((t, d), BF16),

time: 246 us -> 242 us (0.984)
  other arithmetic: 3.35 us -> 0 us
where the time goes in v4:
time: 242 us; the launch traced here: 241 us
  Pallas kernels  239 us (99%)
    pallas_call x1, Pallas kernels, local(): pl.pallas_call(functools.partial(_dispatch_kernel, n, el, cap, nc), out_s...  125 us
    pallas_call x1, Pallas kernels, local(): pl.pallas_call(functools.partial(_return_kernel, n, r, nc), out_shape=jax...  114 us

profile of v4, /device:TPU:97, one launch (start us, length us, event | category | flops | bytes accessed | tf_op | source)
XLA Modules:
  0.0 241.4 jit_solution(2686263274793580725)
XLA Ops:
  0.0 124.9 %shard_map.64 = (bf16[2,4,4,128,1024]{4,3,2,1,0:T(8,128)(2,1)}, bf16[2,4,4,128,1024]{4,3,2,1,0:T(8,128)(2,1)}, bf16[32,256,2048]{2,1,0:T(8,128)(2,1)}, f32[32,16...) custom-call(bf16[256,2048]{1,0:T(8,128)(2,1)} %x_ref.1, s32[8,256]{1,0:T(8,128)} %bitcast.2, f32[8,256]{1,0:T(8,128)} %bitcast.3, ...), custom_call_target="tpu_custom_call" | custom-call | tf_op jit(solution)/shard_map/pallas_call | solution.py:482
  124.9 114.1 %shard_map.65 = bf16[256,2048]{1,0:T(8,128)(2,1)} custom-call(bf16[2,4,4,128,1024]{4,3,2,1,0:T(8,128)(2,1)} %get-tuple-element.9.refs_0_, bf16[2,4,4,128,1024]{4,3,2,1,0:T(8,128)(2,1)} %get-tuple-element.10.refs_1_, f32[32,16,256]{2,1,0:T(8,128)} %get-tuple-element.11.refs_2_, bf16[2,2,4,128,1024]{4,3,2,1,0:T(8,128)(2,1)} %get-tuple-element.12.refs_3_), custom_call_target="tpu_custom_call" | custom-call | tf_op jit(solution)/shard_map/pallas_call | solution.py:502
  239.1 2.3 copy.8
